TPU v7x, 512 devices: a 8x2x16 block of a 8x8x16 slice. The times are simulated.
512 devices in a mesh: grp: 2 (over y), ctx: 32 (over z, core), hd: 8 (over x).
Axes of the slice: x: 8, y: 2, z: 16, core: 2. Of those that a mesh axis runs over, the one named last changes fastest.
The devices are a block of a 8x8x16 slice.
Arguments:
- query: bfloat16 [8192, 4096], P(('grp', 'ctx'), 'hd'), parts along dimension 0, may hold values from -6 to 6
- keys: bfloat16 [8192, 1024], P(('grp', 'ctx'), 'hd'), parts along dimension 0, may hold values from -6 to 6
- values: bfloat16 [8192, 1024], P(('grp', 'ctx'), 'hd'), parts along dimension 0, may hold values from -6 to 6
- m_x: bfloat16 [8192, 8192], P(('grp', 'ctx'), 'hd'), parts along dimension 0, may hold values from -6 to 6
- m_z: bfloat16 [8192, 8192], P(('grp', 'ctx'), 'hd'), parts along dimension 0, may hold values from -6 to 6
- m_b: bfloat16 [8192, 1024], P(('grp', 'ctx'), 'hd'), parts along dimension 0, may hold values from -6 to 6
- m_c: bfloat16 [8192, 1024], P(('grp', 'ctx'), 'hd'), parts along dimension 0, may hold values from -0.5 to 0.5
- dt_raw: bfloat16 [8192, 128], P(('grp', 'ctx'), 'hd'), parts along dimension 0, may hold values from -5 to 204
- dt_bias: float32 [128], P('hd'), may hold values from -0.5 to 0.5
- a_log: float32 [128], P('hd'), may hold values from -10 to 0
- d_skip: float32 [128], P('hd'), may hold values from 0.5 to 2
- norm_gain: float32 [8192], P('hd'), may hold values from 0.5 to 1.5
Outputs:
- context: bfloat16 [8192, 4096], P(('grp', 'ctx'), 'hd'), parts along dimension 0
- mixed: bfloat16 [8192, 8192], P(('grp', 'ctx'), 'hd'), parts along dimension 0
There are 2 independent parts, one for each index of `grp`. A program takes and returns all parts, laid end to end along the dimension named above; an argument that names none is the same for every part. Nothing has to cross between parts.
All inputs are finite; a program needn't handle non-finite values.
Results may differ from a plain program's by a relative error of at most 0.009.
Values may be sent and summed in bfloat16 or wider, within the bound.
No kernel may reach another device: no remote copies, remote signals or barrier semaphores. Data moves between devices by JAX's collectives and lax.ppermute only.
A program may use at most 64 MiB of HBM per device.

v0:
```python
import math
import jax
import jax.numpy as jnp
from jax import lax
from jax.sharding import Mesh
from jax.sharding import PartitionSpec as P

HEAD_SIZE = 128
MP = 64
MN = 128
CTX = ("ctx_0", "ctx_1")
GRP_CTX = ("grp", "ctx_0", "ctx_1")
norm_eps = 1e-05
masked_score = -1e30


def in_order(blocks, dim):
    blocks = jnp.moveaxis(blocks, 0, dim)
    shape = blocks.shape
    return blocks.reshape(*shape[:dim], shape[dim] * shape[dim + 1], *shape[dim + 2 :])


def stacked_from(shard, axes, order):
    blocks = shard
    for k in order:
        blocks = lax.all_gather(blocks, axes[k])
    done = order[::-1]
    back = [done.index(k) for k in range(len(axes))]
    blocks = blocks.transpose(*back, *range(len(axes), blocks.ndim))
    return blocks.reshape(-1, *shard.shape)


def gather_axes(shard, axes, order, dim):
    return in_order(stacked_from(shard, axes, order), dim)


def sent_together(arrays, axis, dim, along):
    ends, at = ([], 0)
    for a in arrays[:-1]:
        at += a.shape[along]
        ends.append(at)
    both = jnp.concatenate(arrays, axis=along)
    return tuple(jnp.split(lax.all_gather(both, axis, axis=dim, tiled=True), ends, axis=along))


def token_position(row_index, tok_rows, ctx_count):
    device = row_index // tok_rows
    within = row_index - device * tok_rows
    half_rows = tok_rows // 2
    second = within >= half_rows
    block_index = jnp.where(second, 2 * ctx_count - 1 - device, device)
    return block_index * half_rows + within - jnp.where(second, half_rows, 0)


def pick_block(total_rows, limit):
    selected = 1
    for candidate in range(1, min(total_rows, limit) + 1):
        if total_rows % candidate == 0:
            selected = candidate
    return selected


def folded_to_sequence(whole, ctx_count):
    half_rows = whole.shape[0] // (2 * ctx_count)
    blocks = whole.reshape((ctx_count, 2, half_rows) + whole.shape[1:])
    return jnp.concatenate([blocks[:, 0], blocks[::-1, 1]], axis=0).reshape(whole.shape)


def attend(query, keys, values):
    tok_rows = query.shape[0]
    ctx_count = lax.axis_size(CTX)
    kv_local = keys.shape[1] // HEAD_SIZE
    heads_per_group = query.shape[1] // keys.shape[1]
    query_heads = query.reshape(tok_rows, kv_local, heads_per_group, HEAD_SIZE)
    own_rows = lax.axis_index(CTX) * tok_rows + jnp.arange(tok_rows, dtype=jnp.int32)
    query_pos = token_position(own_rows, tok_rows, ctx_count)
    scaling = 1.0 / math.sqrt(HEAD_SIZE)
    start_max = jnp.full((kv_local, heads_per_group, tok_rows), masked_score, jnp.float32)
    start_sum = jnp.zeros((kv_local, heads_per_group, tok_rows), jnp.float32)
    start_acc = jnp.zeros((kv_local, heads_per_group, tok_rows, HEAD_SIZE), jnp.float32)
    start = jnp.int32(0)
    key_piece = gather_axes(keys, CTX, (0, 1), 0)
    value_piece = gather_axes(values, CTX, (0, 1), 0)
    piece_rows = key_piece.shape[0]
    rows_per_block = pick_block(piece_rows, 1024)

    def one_block(index, running):
        running_max, running_sum, running_acc = running
        offset = index * rows_per_block
        key_block = lax.dynamic_slice_in_dim(key_piece, offset, rows_per_block, 0).reshape(
            rows_per_block, kv_local, HEAD_SIZE
        )
        value_block = lax.dynamic_slice_in_dim(value_piece, offset, rows_per_block, 0).reshape(
            rows_per_block, kv_local, HEAD_SIZE
        )
        key_pos = token_position(
            start + offset + jnp.arange(rows_per_block, dtype=jnp.int32), tok_rows, ctx_count
        )
        visible = key_pos[None, :] <= query_pos[:, None]
        scores = (
            jnp.einsum("qhgd,khd->hgqk", query_heads, key_block, preferred_element_type=jnp.float32)
            * scaling
        )
        scores = jnp.where(visible, scores, masked_score)
        new_max = jnp.maximum(running_max, jnp.max(scores, axis=-1))
        weights = jnp.where(visible, jnp.exp(scores - new_max[..., None]), 0.0)
        factor = jnp.exp(running_max - new_max)
        new_sum = running_sum * factor + jnp.sum(weights, axis=-1)
        update = jnp.einsum(
            "hgqk,khd->hgqd",
            weights.astype(jnp.bfloat16),
            value_block,
            preferred_element_type=jnp.float32,
        )
        return (new_max, new_sum, running_acc * factor[..., None] + update)

    final_max, final_sum, final_acc = lax.fori_loop(
        0, piece_rows // rows_per_block, one_block, (start_max, start_sum, start_acc)
    )
    averaged = final_acc / final_sum[..., None]
    return jnp.transpose(averaged, (2, 0, 1, 3)).reshape(tok_rows, -1).astype(jnp.bfloat16)


def ssd_block(inputs, steps, rates, b_rows, c_rows):
    intersection = jnp.dot(c_rows, b_rows.T, preferred_element_type=jnp.float32)
    inputs = inputs.astype(jnp.float32)
    b_rows = b_rows.astype(jnp.float32)
    sequence_length = inputs.shape[0]
    running = jnp.cumsum(-steps * rates, axis=0)
    lower = jnp.arange(sequence_length)[:, None] >= jnp.arange(sequence_length)[None, :]
    spread = running[:, None, :] - running[None, :, :]
    decay = jnp.exp(jnp.where(lower[:, :, None], spread, -jnp.inf))
    weights = intersection[:, :, None] * decay * steps[None, :, :]
    inner = jnp.einsum("ijh,jhp->ihp", weights, inputs)
    tail_weight = jnp.exp(running[-1][None, :] - running) * steps
    state = jnp.einsum("jh,jhp,jn->hpn", tail_weight, inputs, b_rows)
    return (inner, state, jnp.exp(running[-1]), jnp.exp(running))


def chain_states(earlier, later):
    return (earlier[0] * later[0], earlier[1] * later[0][..., None, None] + later[1])


def ssd_sequence(inputs, steps, rates, b_rows, c_rows):
    sequence_length, head_count, width = inputs.shape
    block_len = math.gcd(sequence_length, 128)
    count = sequence_length // block_len
    c_blocks = c_rows.reshape(count, block_len, -1)
    inner, state, totals, scaled = jax.vmap(ssd_block, in_axes=(0, 0, None, 0, 0))(
        inputs.reshape(count, block_len, head_count, width),
        steps.reshape(count, block_len, head_count),
        rates,
        b_rows.reshape(count, block_len, -1),
        c_blocks,
    )
    running = lax.associative_scan(chain_states, (totals, state))
    entering = jnp.concatenate([jnp.zeros_like(running[1][:1]), running[1][:-1]], axis=0)
    carried = (
        jnp.einsum("cqn,chpn->cqhp", c_blocks.astype(jnp.float32), entering) * scaled[..., None]
    )
    return (inner + carried).reshape(sequence_length, head_count, width)


def gated_norm(gated_rows, norm_scale, group_count):
    row_count = gated_rows.shape[0]
    widened = (
        lax.optimization_barrier(gated_rows).astype(jnp.float32).reshape(row_count, group_count, -1)
    )
    power = jnp.mean(widened * widened, axis=-1, keepdims=True)
    return ((widened * lax.rsqrt(power + norm_eps)).reshape(row_count, -1) * norm_scale).astype(
        jnp.bfloat16
    )


def body(query, keys, values, m_x, m_z, m_b, m_c, dt_raw, dt_bias, a_log, d_skip, norm_gain):
    ctx_count = lax.axis_size(CTX)
    context_fold = attend(query, keys, values)
    groups_here = m_b.shape[1] // MN
    rates = jnp.exp(a_log)
    x_cols, z_cols, context_cols = (
        lax.all_to_all(m_x, CTX, split_axis=1, concat_axis=0, tiled=True),
        lax.all_to_all(m_z, CTX, split_axis=1, concat_axis=0, tiled=True),
        lax.all_to_all(context_fold, CTX, split_axis=1, concat_axis=0, tiled=True),
    )
    dt_whole, b_whole, c_whole = sent_together((dt_raw, m_b, m_c), CTX, 0, 1)
    x_cols = folded_to_sequence(x_cols, ctx_count)
    z_cols = folded_to_sequence(z_cols, ctx_count)
    context_cols = folded_to_sequence(context_cols, ctx_count)
    dt_whole = folded_to_sequence(dt_whole, ctx_count)
    b_whole = folded_to_sequence(b_whole, ctx_count)
    c_whole = folded_to_sequence(c_whole, ctx_count)
    sequence_length = x_cols.shape[0]
    width = x_cols.shape[1]
    sub_width = min(width, MP)
    head_count = width // sub_width
    first_head = lax.axis_index(CTX) * width // MP
    step_mine = jax.nn.softplus(
        lax.dynamic_slice_in_dim(dt_whole, first_head, head_count, 1).astype(jnp.float32)
        + lax.dynamic_slice_in_dim(dt_bias, first_head, head_count, 0)
    )
    rate_mine = lax.dynamic_slice_in_dim(rates, first_head, head_count, 0)
    skip_mine = lax.dynamic_slice_in_dim(d_skip, first_head, head_count, 0)
    x_mine = x_cols.reshape(sequence_length, head_count, sub_width)
    outputs = ssd_sequence(x_mine, step_mine, rate_mine, b_whole, c_whole)
    outputs = outputs + skip_mine[None, :, None] * x_mine.astype(jnp.float32)
    gated = (
        outputs.reshape(sequence_length, width) * jax.nn.silu(z_cols.astype(jnp.float32))
    ).astype(jnp.bfloat16)
    gated_rows, context = (
        lax.all_to_all(gated, CTX, split_axis=0, concat_axis=1, tiled=True),
        lax.all_to_all(context_cols, CTX, split_axis=0, concat_axis=1, tiled=True),
    )
    mixed = gated_norm(gated_rows, norm_gain, groups_here)
    return (context, mixed)


def solution(mesh):
    split = Mesh(
        mesh.devices.reshape(mesh.shape["grp"], 16, 2, mesh.shape["hd"]),
        ("grp", "ctx_0", "ctx_1", "hd"),
    )
    return jax.shard_map(
        body,
        mesh=split,
        in_specs=(
            P(GRP_CTX, "hd"),
            P(GRP_CTX, "hd"),
            P(GRP_CTX, "hd"),
            P(GRP_CTX, "hd"),
            P(GRP_CTX, "hd"),
            P(GRP_CTX, "hd"),
            P(GRP_CTX, "hd"),
            P(GRP_CTX, "hd"),
            P("hd"),
            P("hd"),
            P("hd"),
            P("hd"),
        ),
        out_specs=(P(GRP_CTX, "hd"), P(GRP_CTX, "hd")),
        check_vma=False,
    )
```

profile of v0, /device:TPU:65, one launch (start us, length us, event | category | flops | bytes accessed | tf_op | source)
XLA Modules:
  0.0 289.9 jit_solution(6494011130567231543)
XLA Ops:
  7.3 67.5 %all-gather = bf16[2048,128]{1,0:T(8,128)(2,1)} all-gather(bf16[128,128]{1,0:T(8,128)(2,1)} %param.15), channel_id=2, replica_groups=mesh['grp'=2,'ctx_0'=16,'ctx_1'=2,'hd'=8] {'ctx_0'}, dimensions={0}, use_global_device_ids=true | all-gather | bytes 557056 | tf_op jit(solution)/shard_map/all_gather | solution.py:26
  75.0 25.6 %all-gather.2 = bf16[2048,128]{1,0:T(8,128)(2,1)} all-gather(bf16[128,128]{1,0:T(8,128)(2,1)} %param.16), channel_id=4, replica_groups=mesh['grp'=2,'ctx_0'=16,'ctx_1'=2,'hd'=8] {'ctx_0'}, dimensions={0}, use_global_device_ids=true | all-gather | bytes 557056 | tf_op jit(solution)/shard_map/all_gather | solution.py:26
  101.5 18.2 %all-to-all-start.2 = ((bf16[128,32,32]{0,2,1:T(8,128)(2,1)}), bf16[128,32,32]{0,2,1:T(8,128)(2,1)S(1)}, u32[]{:S(2)}, u32[]{:S(2)}) async-start(bf16[128,32,32]{0,2,1:T(8,128)(2,1)} %bitcast.17), calls=%async_computation.2 | async-start | bytes 524288 | tf_op jit(solution)/shard_map/all_to_all | solution.py:181
  124.4 17.4 %all-to-all-done.2 = bf16[128,32,32]{0,2,1:T(8,128)(2,1)S(1)} async-done(((bf16[128,32,32]{0,2,1:T(8,128)(2,1)}), bf16[128,32,32]{0,2,1:T(8,128)(2,1)S(1)}, u32[]{:S(2)}, u32[]{:S(2)}) %all-to-all-start.2) | async-done | bytes 262176 | tf_op jit(solution)/shard_map/all_to_all | solution.py:181
  141.9 5.0 %all-to-all-start.3 = ((bf16[128,32,32]{0,2,1:T(8,128)(2,1)}), bf16[128,32,32]{0,2,1:T(8,128)(2,1)}, u32[]{:S(2)}, u32[]{:S(2)}) async-start(bf16[128,32,32]{0,2,1:T(8,128)(2,1)} %bitcast.54), calls=%async_computation.3 | async-start | bytes 524288 | tf_op jit(solution)/shard_map/all_to_all | solution.py:182
  149.9 1.4 copy.146
  151.3 2.4 copy.148
  153.7 16.5 %while.20 = (s32[]{:T(128)}, f32[1,4,128]{2,1,0:T(4,128)S(1)}, f32[1,4,128]{2,1,0:T(4,128)S(1)}, f32[1,4,128,128]{3,2,1,0:T(8,128)}, bf16[4096,128]{1,0:T(8,128)...) while((s32[]{:T(128)}, f32[1,4,128]{2,1,0:T(4,128)S(1)}, ...), condition=%wide.region_3.4_spmd.clone, body=%wide.region_0.3_spmd.clone.sunk | while | flops 275610752 | bytes 10134783 | solution.py:117
  155.3 1.8 fusion.98
  159.4 1.8 fusion.98
  163.6 1.8 fusion.98
  167.7 1.8 fusion.98
  170.2 1.1 copy.150
  172.0 12.6 %all-to-all-start = ((bf16[128,32,16]{0,2,1:T(8,128)(2,1)}), bf16[128,32,16]{0,2,1:T(8,128)(2,1)S(1)}, u32[]{:S(2)}, u32[]{:S(2)}) async-start(bf16[128,32,16]{0,2,1:T(8,128)(2,1)} %bitcast.11), calls=%async_computation | async-start | bytes 262144 | tf_op jit(solution)/shard_map/all_to_all | solution.py:183
  184.6 1.2 pad_maximum_fusion.2
  186.0 1.3 reshape.332
  189.9 11.9 %all-to-all-done = bf16[128,32,16]{0,2,1:T(8,128)(2,1)S(1)} async-done(((bf16[128,32,16]{0,2,1:T(8,128)(2,1)}), bf16[128,32,16]{0,2,1:T(8,128)(2,1)S(1)}, u32[]{:S(2)}, u32[]{:S(2)}) %all-to-all-start) | async-done | bytes 131104 | tf_op jit(solution)/shard_map/all_to_all | solution.py:183
  203.5 5.5 %all-to-all-start.1 = ((bf16[32,128,16]{1,2,0:T(8,128)(2,1)}), bf16[32,128,16]{1,2,0:T(8,128)(2,1)}, u32[]{:S(2)}, u32[]{:S(2)}) async-start(bf16[32,128,16]{1,2,0:T(8,128)(2,1)} %copy.153), calls=%async_computation.1 | async-start | bytes 262144 | tf_op jit(solution)/shard_map/all_to_all | solution.py:211
  209.0 4.6 %all-gather.8.cloned.1.call-done = bf16[4096,272]{1,0:T(8,128)(2,1)} async-done(((bf16[128,272]{1,0:T(8,128)(2,1)}), bf16[4096,272]{1,0:T(8,128)(2,1)}) %all-gather.8.cloned.1.call-update) | async-done | bytes 2228240 | tf_op jit(solution)/shard_map/all_gather | solution.py:43
  213.6 1.2 slice-done
  216.5 1.4 negate_multiply_fusion
  218.0 2.9 copy.166
  220.8 1.8 fusion.77
  222.6 1.3 copy.167
  226.8 2.9 %fusion.71 = (bf16[4096,128]{1,0:T(8,128)(2,1)S(1)}, bf16[4096,128]{1,0:T(8,128)(2,1)S(1)}) fusion(bf16[4096,272]{1,0:T(8,128)(2,1)} %all-gather.8.cloned.1.call-done), kind=kLoop, calls=%fused_computation.137 | loop fusion | bytes 4194304 | tf_op jit(solution)/shard_map/split | solution.py:43
  238.1 5.8 %pad.103 = f32[32,1,32,128]{3,2,0,1:T(8,128)S(1)} pad(f32[16,1,32,128]{3,2,0,1:T(8,128)} %add.239, f32[]{:T(128)} %constant.191.clone.1), padding=1_0_1x0_0_0x0_0_0x0_0_0 | pad | bytes 786436
  243.9 1.1 pad_maximum_fusion
  245.0 3.5 %fusion.41 = f32[32,128,1,32]{1,3,0,2:T(8,128)} fusion(bf16[32,128,128]{2,1,0:T(8,128)(2,1)} %bitcast.209, bf16[32,128,128]{2,1,0:T(8,128)(2,1)S(1)} %bitcast.197, f32[32,128]{1,0:T(8,128)S(1)} %bitcast.228, f32[32,128]{1,0:T(8,128)S(1)} %bitcast.226, pred[128,128]{1,0:T(8,128)(4,1)S(1)} %copy-done.13, bf16[32,128,32]{1,0,2:T(8,128)(2,1)S(1)} %copy-done.1), kind=kOutput, calls=%fused_computation.63 | convolution fusion | flops 169869312 | bytes 2932736 | tf_op jit(solution)/shard_map/vmap(ijh,jhp->ihp)/dot_general | solution.py:134
  248.6 3.2 %fusion.48 = bf16[32,128,32]{1,2,0:T(8,128)(2,1)} fusion(f32[32,128,1,32]{1,3,0,2:T(8,128)} %fusion.41, bf16[32,128,128]{2,1,0:T(8,128)(2,1)S(1)} %bitcast.210, f32[32,128,32]{1,0,2:T(8,128)} %reshape.333, bf16[31,1,32,128]{3,2,0,1:T(8,128)(2,1)S(1)} %slice_add_fusion.5, f32[]{:T(128)} %bitcast.53, f32[32,128]{1,0:T(8,128)S(1)} %copy-done.14, ...), kind=kOutput, calls=%fused_computation.68 | convolution fusion | flops 34996224 | bytes 2891780 | tf_op jit(solution)/shard_map/cqn,chpn->cqhp/dot_general | solution.py:159
  251.8 8.3 %all-to-all-start.4 = ((bf16[32,128,32]{1,2,0:T(8,128)(2,1)}), bf16[32,128,32]{1,2,0:T(8,128)(2,1)S(1)}, u32[]{:S(2)}, u32[]{:S(2)}) async-start(bf16[32,128,32]{1,2,0:T(8,128)(2,1)} %fusion.48), calls=%async_computation.4 | async-start | bytes 524288 | tf_op jit(solution)/shard_map/all_to_all | solution.py:210
  260.1 1.7 copy.176
  261.8 20.4 %all-to-all-done.4 = bf16[32,128,32]{1,2,0:T(8,128)(2,1)S(1)} async-done(((bf16[32,128,32]{1,2,0:T(8,128)(2,1)}), bf16[32,128,32]{1,2,0:T(8,128)(2,1)S(1)}, u32[]{:S(2)}, u32[]{:S(2)}) %all-to-all-start.4) | async-done | bytes 262176 | tf_op jit(solution)/shard_map/all_to_all | solution.py:210
  (195 shorter events, 37.0 us)
Async XLA Ops:
  7.2 93.4 %copy-start.3 = (bf16[128,1024]{1,0:T(8,128)(2,1)S(1)}, bf16[128,1024]{1,0:T(8,128)(2,1)}, u32[]{:S(2)}) copy-start(bf16[128,1024]{1,0:T(8,128)(2,1)} %param.17) | copy-start | bytes 786436
  7.2 112.6 %copy-start.16 = (bf16[128,16]{0,1:T(8,128)(2,1)S(1)}, bf16[128,16]{0,1:T(8,128)(2,1)}, u32[]{:S(2)}) copy-start(bf16[128,16]{0,1:T(8,128)(2,1)} %param.21) | copy-start | bytes 12292
  7.2 112.8 %copy-start.11 = (bf16[128,128]{1,0:T(8,128)(2,1)S(1)}, bf16[128,128]{1,0:T(8,128)(2,1)}, u32[]{:S(2)}) copy-start(bf16[128,128]{1,0:T(8,128)(2,1)} %param.20) | copy-start | bytes 98308
  7.2 112.7 %copy-start.12 = (bf16[128,128]{1,0:T(8,128)(2,1)S(1)}, bf16[128,128]{1,0:T(8,128)(2,1)}, u32[]{:S(2)}) copy-start(bf16[128,128]{1,0:T(8,128)(2,1)} %param.19) | copy-start | bytes 98308
  7.2 113.6 %copy-start.7 = (bf16[128,512]{1,0:T(8,128)(2,1)S(1)}, bf16[128,512]{1,0:T(8,128)(2,1)}, u32[]{:S(2)}) copy-start(bf16[128,512]{1,0:T(8,128)(2,1)} %param.14) | copy-start | bytes 393220
  7.2 113.9 %copy-start.17 = (f32[16]{0:T(128)S(1)}, f32[16]{0:T(128)}, u32[]{:S(2)}) copy-start(f32[16]{0:T(128)} %param.23) | copy-start | bytes 196
  7.2 114.5 %copy-start.18 = (f32[16]{0:T(128)S(1)}, f32[16]{0:T(128)}, u32[]{:S(2)}) copy-start(f32[16]{0:T(128)} %param.22) | copy-start | bytes 196
  7.2 115.2 %copy-start.4 = (bf16[128,1024]{1,0:T(8,128)(2,1)S(1)}, bf16[128,1024]{1,0:T(8,128)(2,1)}, u32[]{:S(2)}) copy-start(bf16[128,1024]{1,0:T(8,128)(2,1)} %param.18) | copy-start | bytes 786436
  7.3 142.6 %all-gather.10.cloned.1.call-start = ((), (), s32[]{:S(2)}) async-start(), calls=%async_computation.6 | async-start | bytes 1572864 | tf_op jit(solution)/shard_map/all_gather | solution.py:26
  74.8 48.4 %copy-start.19 = (f32[16]{0:T(128)S(1)}, f32[16]{0:T(128)}, u32[]{:S(2)}) copy-start(f32[16]{0:T(128)} %param.24) | copy-start | bytes 196
  74.9 76.4 %all-gather.12.cloned.1.call-start = ((), (), s32[]{:S(2)}) async-start(), calls=%async_computation.7 | async-start | bytes 1572864 | tf_op jit(solution)/shard_map/all_gather | solution.py:26
  101.5 40.4 %all-to-all-start.2 = ((bf16[128,32,32]{0,2,1:T(8,128)(2,1)}), bf16[128,32,32]{0,2,1:T(8,128)(2,1)S(1)}, u32[]{:S(2)}, u32[]{:S(2)}) async-start(bf16[128,32,32]{0,2,1:T(8,128)(2,1)} %bitcast.17), calls=%async_computation.2 | async-start | bytes 524288 | tf_op jit(solution)/shard_map/all_to_all | solution.py:181
  119.7 93.9 %all-gather.8.cloned.1.call-start = ((), (), s32[]{:S(2)}) async-start(), calls=%async_computation.5 | async-start | bytes 3244032 | tf_op jit(solution)/shard_map/all_gather | solution.py:43
  141.9 30.1 %all-to-all-start.3 = ((bf16[128,32,32]{0,2,1:T(8,128)(2,1)}), bf16[128,32,32]{0,2,1:T(8,128)(2,1)}, u32[]{:S(2)}, u32[]{:S(2)}) async-start(bf16[128,32,32]{0,2,1:T(8,128)(2,1)} %bitcast.54), calls=%async_computation.3 | async-start | bytes 524288 | tf_op jit(solution)/shard_map/all_to_all | solution.py:182
  154.4 1.0 copy-start.5
  157.1 0.7 copy-start.6
  158.5 1.0 copy-start.5
  162.6 1.0 copy-start.5
  166.8 1.0 copy-start.5
  172.0 29.9 %all-to-all-start = ((bf16[128,32,16]{0,2,1:T(8,128)(2,1)}), bf16[128,32,16]{0,2,1:T(8,128)(2,1)S(1)}, u32[]{:S(2)}, u32[]{:S(2)}) async-start(bf16[128,32,16]{0,2,1:T(8,128)(2,1)} %bitcast.11), calls=%async_computation | async-start | bytes 262144 | tf_op jit(solution)/shard_map/all_to_all | solution.py:183
  186.0 44.7 %copy-start = (bf16[32,128,32]{1,0,2:T(8,128)(2,1)}, bf16[32,128,32]{1,0,2:T(8,128)(2,1)S(1)}, u32[]{:S(2)}) copy-start(bf16[32,128,32]{1,0,2:T(8,128)(2,1)S(1)} %reshape.325) | copy-start | bytes 786436
  203.5 48.3 %all-to-all-start.1 = ((bf16[32,128,16]{1,2,0:T(8,128)(2,1)}), bf16[32,128,16]{1,2,0:T(8,128)(2,1)}, u32[]{:S(2)}, u32[]{:S(2)}) async-start(bf16[32,128,16]{1,2,0:T(8,128)(2,1)} %copy.153), calls=%async_computation.1 | async-start | bytes 262144 | tf_op jit(solution)/shard_map/all_to_all | solution.py:211
  213.6 1.2 slice-start
  218.0 12.2 %copy-start.9 = (f32[4096,1]{0,1:T(1,128)}, f32[4096,1]{0,1:T(1,128)S(1)}, u32[]{:S(2)}) copy-start(f32[4096,1]{0,1:T(1,128)S(1)} %get-tuple-element.305) | copy-start | bytes 49156
  234.9 3.0 %copy-start.8 = (f32[1,1,32,128]{3,2,0,1:T(8,128)S(1)}, f32[1,1,32,128]{3,2,0,1:T(8,128)}, u32[]{:S(2)}) copy-start(f32[1,1,32,128]{3,2,0,1:T(8,128)} %slice_bitcast_fusion.4) | copy-start | bytes 49156
  237.9 7.1 %copy-start.1 = (bf16[32,128,32]{1,0,2:T(8,128)(2,1)S(1)}, bf16[32,128,32]{1,0,2:T(8,128)(2,1)}, u32[]{:S(2)}) copy-start(bf16[32,128,32]{1,0,2:T(8,128)(2,1)} %copy-done) | copy-start | bytes 786436
  237.9 7.1 %copy-start.10 = (f32[4096,1]{0,1:T(1,128)S(1)}, f32[4096,1]{0,1:T(1,128)}, u32[]{:S(2)}) copy-start(f32[4096,1]{0,1:T(1,128)} %copy-done.9) | copy-start | bytes 49156
  237.9 7.1 %copy-start.13 = (pred[128,128]{1,0:T(8,128)(4,1)S(1)}, pred[128,128]{1,0:T(8,128)(4,1)}, u32[]{:S(2)}) copy-start(pred[128,128]{1,0:T(8,128)(4,1)} %iota_compare_fusion) | copy-start | bytes 49156
  245.0 3.6 %copy-start.2 = (bf16[64,64,128]{2,1,0:T(8,128)(2,1)S(1)}, bf16[64,64,128]{2,1,0:T(8,128)(2,1)}, u32[]{:S(2)}) copy-start(bf16[64,64,128]{2,1,0:T(8,128)(2,1)} %pad_maximum_fusion) | copy-start | bytes 3145732
  245.0 3.6 %copy-start.14 = (f32[32,128]{1,0:T(8,128)S(1)}, f32[32,128]{1,0:T(8,128)}, u32[]{:S(2)}) copy-start(f32[32,128]{1,0:T(8,128)} %get-tuple-element.326) | copy-start | bytes 49156
  248.6 33.9 %copy-start.15 = (f32[1024]{0:T(1024)S(1)}, f32[1024]{0:T(1024)}, u32[]{:S(2)}) copy-start(f32[1024]{0:T(1024)} %param.25) | copy-start | bytes 12292
  251.8 30.4 %all-to-all-start.4 = ((bf16[32,128,32]{1,2,0:T(8,128)(2,1)}), bf16[32,128,32]{1,2,0:T(8,128)(2,1)S(1)}, u32[]{:S(2)}, u32[]{:S(2)}) async-start(bf16[32,128,32]{1,2,0:T(8,128)(2,1)} %fusion.48), calls=%async_computation.4 | async-start | bytes 524288 | tf_op jit(solution)/shard_map/all_to_all | solution.py:210
  (3 other events, 2.1 us)
Sparse Core Ops, SparseCore 0:
  75.0 23.9 all-gather.9
  101.1 30.5 all-gather.11
  133.9 79.7 all-gather.7
where the time goes:
time: 292 us; the launch traced here: 290 us
  blocking collectives  93.1 us (32%)
  waiting for transfers between devices  54.5 us (19%)
  starting transfers between devices  49.8 us (17%)
  local copies, waits for them, and re-layouts  44.6 us (15%)
  other arithmetic  17.3 us (6%)
  matrix products  15.8 us (5%)
  between operations  14.5 us (5%)
    all_gather x2, blocking collectives, stacked_from(): blocks = lax.all_gather(blocks, axes[k])  93.1 us
    all_to_all x1, waiting for transfers between devices, body(): lax.all_to_all(gated, CTX, split_axis=0, concat_axis=1, tiled=True)  20.4 us
    all_to_all x1, starting transfers between devices, body(): lax.all_to_all(m_x, CTX, split_axis=1, concat_axis=0, tiled=True)  18.2 us
    all_to_all x1, waiting for transfers between devices, body(): lax.all_to_all(m_x, CTX, split_axis=1, concat_axis=0, tiled=True)  17.4 us
    all_to_all x1, starting transfers between devices, body(): lax.all_to_all(context_fold, CTX, split_axis=1, concat_axis=0, tiled=True)  12.6 us
    unnamed x50, local copies, waits for them, and re-layouts  12.3 us
    all_to_all x1, waiting for transfers between devices, body(): lax.all_to_all(context_fold, CTX, split_axis=1, concat_axis=0, tiled=True)  11.9 us
    all_to_all x1, starting transfers between devices, body(): lax.all_to_all(gated, CTX, split_axis=0, concat_axis=1, tiled=True)  8.33 us
  transfers between devices with their start and end apart: 8, of which 4 were waited for; matrix products, arithmetic and copies ran while one was open for 24% of the time, Pallas kernels for 0%

commit v1 on v0

--- a/solution.py
+++ b/solution.py
@@ -12,6 +12,13 @@
 GRP_CTX = ("grp", "ctx_0", "ctx_1")
 norm_eps = 1e-05
 masked_score = -1e30
+
+
+def stacked_exchange(shard, axis, split, join):
+    size = lax.axis_size(axis)
+    pieces = jnp.stack(jnp.split(shard, size, axis=split), axis=0)
+    pieces = lax.all_to_all(pieces, axis, split_axis=0, concat_axis=0)
+    return jnp.concatenate(pieces, axis=join)
 
 
 def in_order(blocks, dim):
@@ -178,7 +185,7 @@
     groups_here = m_b.shape[1] // MN
     rates = jnp.exp(a_log)
     x_cols, z_cols, context_cols = (
-        lax.all_to_all(m_x, CTX, split_axis=1, concat_axis=0, tiled=True),
+        stacked_exchange(m_x, CTX, 1, 0),
         lax.all_to_all(m_z, CTX, split_axis=1, concat_axis=0, tiled=True),
         lax.all_to_all(context_fold, CTX, split_axis=1, concat_axis=0, tiled=True),
     )

time: 292 us -> 313 us (1.072)
  local copies, waits for them, and re-layouts: 44.6 us -> 66 us
  starting transfers between devices: 49.8 us -> 54.4 us
  waiting for transfers between devices: 54.5 us -> 50 us
    unnamed x50 -> x112, local copies, waits for them, and re-layouts: 12.3 us -> 32.7 us
    all_gather x1, waiting for transfers between devices: 4.58 us -> 0.02 us  [sent_together(): lax.all_gather(both, axis, axis=dim, tiled=True)]
    all_to_all x1, starting transfers between devices: 8.33 us -> 12.7 us  [body(): lax.all_to_all(gated, CTX, split_axis=0, concat_axis=1, tiled=True)]
  transfers between devices with their start and end apart: 8 -> 8, of which waited for: 4 -> 3; matrix products, arithmetic and copies ran while one was open for 24% -> 30% of each run, Pallas kernels for 0% -> 0%
where the time goes in v1:
time: 313 us; the launch traced here: 311 us
  blocking collectives  93 us (30%)
  local copies, waits for them, and re-layouts  66 us (21%)
  starting transfers between devices  54.4 us (17%)
  waiting for transfers between devices  50 us (16%)
  other arithmetic  17.3 us (6%)
  matrix products  15.9 us (5%)
  between operations  14.6 us (5%)
    all_gather x2, blocking collectives, stacked_from(): blocks = lax.all_gather(blocks, axes[k])  93 us
    unnamed x112, local copies, waits for them, and re-layouts  32.7 us
    all_to_all x1, waiting for transfers between devices, body(): lax.all_to_all(gated, CTX, split_axis=0, concat_axis=1, tiled=True)  20.4 us
    all_to_all x1, starting transfers between devices, stacked_exchange(): pieces = lax.all_to_all(pieces, axis, split_axis=0, concat_axis=0)  18.2 us
    all_to_all x1, waiting for transfers between devices, stacked_exchange(): pieces = lax.all_to_all(pieces, axis, split_axis=0, concat_axis=0)  17.4 us
    all_to_all x1, starting transfers between devices, body(): lax.all_to_all(context_fold, CTX, split_axis=1, concat_axis=0, tiled=True)  12.7 us
    all_to_all x1, starting transfers between devices, body(): lax.all_to_all(gated, CTX, split_axis=0, concat_axis=1, tiled=True)  12.7 us
    all_to_all x1, waiting for transfers between devices, body(): lax.all_to_all(context_fold, CTX, split_axis=1, concat_axis=0, tiled=True)  12 us
  transfers between devices with their start and end apart: 8, of which 3 were waited for; matrix products, arithmetic and copies ran while one was open for 30% of the time, Pallas kernels for 0%

profile of v1, /device:TPU:65, one launch (start us, length us, event | category | flops | bytes accessed | tf_op | source)
XLA Modules:
  0.0 311.5 jit_solution(3465666563560162243)
XLA Ops:
  7.3 67.4 %all-gather = bf16[2048,128]{1,0:T(8,128)(2,1)} all-gather(bf16[128,128]{1,0:T(8,128)(2,1)} %param.15), channel_id=2, replica_groups=mesh['grp'=2,'ctx_0'=16,'ctx_1'=2,'hd'=8] {'ctx_0'}, dimensions={0}, use_global_device_ids=true | all-gather | bytes 557056 | tf_op jit(solution)/shard_map/all_gather | solution.py:33
  74.8 25.6 %all-gather.2 = bf16[2048,128]{1,0:T(8,128)(2,1)} all-gather(bf16[128,128]{1,0:T(8,128)(2,1)} %param.16), channel_id=4, replica_groups=mesh['grp'=2,'ctx_0'=16,'ctx_1'=2,'hd'=8] {'ctx_0'}, dimensions={0}, use_global_device_ids=true | all-gather | bytes 557056 | tf_op jit(solution)/shard_map/all_gather | solution.py:33
  122.8 18.2 %all-to-all-start.2 = ((bf16[32,128,32]{1,2,0:T(8,128)(2,1)}), bf16[32,128,32]{1,2,0:T(8,128)(2,1)S(1)}, u32[]{:S(2)}, u32[]{:S(2)}) async-start(bf16[32,128,32]{1,2,0:T(8,128)(2,1)} %constant_dynamic-update-slice_fusion), calls=%async_computation.2 | async-start | bytes 524288 | tf_op jit(solution)/shard_map/all_to_all | solution.py:20
  145.8 17.4 %all-to-all-done.2 = bf16[32,128,32]{1,2,0:T(8,128)(2,1)S(1)} async-done(((bf16[32,128,32]{1,2,0:T(8,128)(2,1)}), bf16[32,128,32]{1,2,0:T(8,128)(2,1)S(1)}, u32[]{:S(2)}, u32[]{:S(2)}) %all-to-all-start.2) | async-done | bytes 262176 | tf_op jit(solution)/shard_map/all_to_all | solution.py:20
  163.2 4.9 %all-to-all-start.3 = ((bf16[128,32,32]{0,2,1:T(8,128)(2,1)}), bf16[128,32,32]{0,2,1:T(8,128)(2,1)}, u32[]{:S(2)}, u32[]{:S(2)}) async-start(bf16[128,32,32]{0,2,1:T(8,128)(2,1)} %bitcast.84), calls=%async_computation.3 | async-start | bytes 524288 | tf_op jit(solution)/shard_map/all_to_all | solution.py:189
  170.2 1.0 copy.329
  171.2 1.3 copy.207
  172.6 2.4 copy.209
  174.9 16.5 %while.20 = (s32[]{:T(128)}, f32[1,4,128]{2,1,0:T(4,128)S(1)}, f32[1,4,128]{2,1,0:T(4,128)S(1)}, f32[1,4,128,128]{3,2,1,0:T(8,128)}, bf16[4096,128]{1,0:T(8,128)...) while((s32[]{:T(128)}, f32[1,4,128]{2,1,0:T(4,128)S(1)}, ...), condition=%wide.region_3.4_spmd.clone, body=%wide.region_0.3_spmd.clone.sunk | while | flops 275610752 | bytes 10134783 | solution.py:124
  176.6 1.8 fusion.100
  180.7 1.8 fusion.100
  184.9 1.8 fusion.100
  189.0 1.8 fusion.100
  191.4 1.1 copy.211
  193.2 12.7 %all-to-all-start = ((bf16[128,32,16]{0,2,1:T(8,128)(2,1)}), bf16[128,32,16]{0,2,1:T(8,128)(2,1)S(1)}, u32[]{:S(2)}, u32[]{:S(2)}) async-start(bf16[128,32,16]{0,2,1:T(8,128)(2,1)} %bitcast.11), calls=%async_computation | async-start | bytes 262144 | tf_op jit(solution)/shard_map/all_to_all | solution.py:190
  205.9 1.2 pad_maximum_fusion.2
  207.4 1.3 reshape.324
  211.3 12.0 %all-to-all-done = bf16[128,32,16]{0,2,1:T(8,128)(2,1)S(1)} async-done(((bf16[128,32,16]{0,2,1:T(8,128)(2,1)}), bf16[128,32,16]{0,2,1:T(8,128)(2,1)S(1)}, u32[]{:S(2)}, u32[]{:S(2)}) %all-to-all-start) | async-done | bytes 131104 | tf_op jit(solution)/shard_map/all_to_all | solution.py:190
  225.0 5.6 %all-to-all-start.1 = ((bf16[32,128,16]{1,2,0:T(8,128)(2,1)}), bf16[32,128,16]{1,2,0:T(8,128)(2,1)}, u32[]{:S(2)}, u32[]{:S(2)}) async-start(bf16[32,128,16]{1,2,0:T(8,128)(2,1)} %copy.214), calls=%async_computation.1 | async-start | bytes 262144 | tf_op jit(solution)/shard_map/all_to_all | solution.py:218
  230.6 1.2 slice-done
  233.5 1.4 negate_multiply_fusion
  234.9 2.9 copy.258
  237.7 1.8 fusion.79
  239.5 1.3 copy.259
  243.7 2.9 fusion.71
  255.2 5.8 %pad.103 = f32[32,1,32,128]{3,2,0,1:T(8,128)S(1)} pad(f32[16,1,32,128]{3,2,0,1:T(8,128)} %add.239, f32[]{:T(128)} %constant.191.clone.1), padding=1_0_1x0_0_0x0_0_0x0_0_0 | pad | bytes 786436
  261.0 1.1 pad_maximum_fusion
  262.1 3.5 %fusion.41 = f32[32,128,1,32]{1,3,0,2:T(8,128)} fusion(bf16[32,128,128]{2,1,0:T(8,128)(2,1)} %bitcast.270, bf16[32,128,128]{2,1,0:T(8,128)(2,1)S(1)} %bitcast.259, f32[32,128]{1,0:T(8,128)S(1)} %bitcast.289, f32[32,128]{1,0:T(8,128)S(1)} %bitcast.287, pred[128,128]{1,0:T(8,128)(4,1)S(1)} %copy-done.13, bf16[32,128,32]{1,0,2:T(8,128)(2,1)S(1)} %copy-done.2), kind=kOutput, calls=%fused_computation.63 | convolution fusion | flops 169869312 | bytes 2932736 | tf_op jit(solution)/shard_map/vmap(ijh,jhp->ihp)/dot_general | solution.py:141
  265.7 3.3 %fusion.48 = bf16[32,128,32]{1,2,0:T(8,128)(2,1)} fusion(f32[32,128,1,32]{1,3,0,2:T(8,128)} %fusion.41, bf16[32,128,128]{2,1,0:T(8,128)(2,1)S(1)} %bitcast.271, f32[32,128,32]{1,0,2:T(8,128)} %reshape.325, bf16[31,1,32,128]{3,2,0,1:T(8,128)(2,1)S(1)} %slice_add_fusion.5, f32[]{:T(128)} %bitcast.83, f32[32,128]{1,0:T(8,128)S(1)} %copy-done.14, ...), kind=kOutput, calls=%fused_computation.68 | convolution fusion | flops 34996224 | bytes 2891780 | tf_op jit(solution)/shard_map/cqn,chpn->cqhp/dot_general | solution.py:166
  269.0 12.7 %all-to-all-start.4 = ((bf16[32,128,32]{1,2,0:T(8,128)(2,1)}), bf16[32,128,32]{1,2,0:T(8,128)(2,1)S(1)}, u32[]{:S(2)}, u32[]{:S(2)}) async-start(bf16[32,128,32]{1,2,0:T(8,128)(2,1)} %fusion.48), calls=%async_computation.4 | async-start | bytes 524288 | tf_op jit(solution)/shard_map/all_to_all | solution.py:217
  281.7 1.7 copy.268
  283.4 20.4 %all-to-all-done.4 = bf16[32,128,32]{1,2,0:T(8,128)(2,1)S(1)} async-done(((bf16[32,128,32]{1,2,0:T(8,128)(2,1)}), bf16[32,128,32]{1,2,0:T(8,128)(2,1)S(1)}, u32[]{:S(2)}, u32[]{:S(2)}) %all-to-all-start.4) | async-done | bytes 262176 | tf_op jit(solution)/shard_map/all_to_all | solution.py:217
  (260 shorter events, 57.7 us)
Async XLA Ops:
  7.2 93.2 %copy-start = (bf16[128,1024]{1,0:T(8,128)(2,1)S(1)}, bf16[128,1024]{1,0:T(8,128)(2,1)}, u32[]{:S(2)}) copy-start(bf16[128,1024]{1,0:T(8,128)(2,1)} %param.17) | copy-start | bytes 786436
  7.2 164.1 %all-gather.10.cloned.1.call-start = ((), (), s32[]{:S(2)}) async-start(), calls=%async_computation.6 | async-start | bytes 1572864 | tf_op jit(solution)/shard_map/all_gather | solution.py:33
  74.7 97.9 %all-gather.12.cloned.1.call-start = ((), (), s32[]{:S(2)}) async-start(), calls=%async_computation.7 | async-start | bytes 1572864 | tf_op jit(solution)/shard_map/all_gather | solution.py:33
  100.4 40.7 %copy-start.16 = (bf16[128,16]{0,1:T(8,128)(2,1)S(1)}, bf16[128,16]{0,1:T(8,128)(2,1)}, u32[]{:S(2)}) copy-start(bf16[128,16]{0,1:T(8,128)(2,1)} %param.21) | copy-start | bytes 12292
  100.4 40.9 %copy-start.11 = (bf16[128,128]{1,0:T(8,128)(2,1)S(1)}, bf16[128,128]{1,0:T(8,128)(2,1)}, u32[]{:S(2)}) copy-start(bf16[128,128]{1,0:T(8,128)(2,1)} %param.20) | copy-start | bytes 98308
  100.5 40.8 %copy-start.12 = (bf16[128,128]{1,0:T(8,128)(2,1)S(1)}, bf16[128,128]{1,0:T(8,128)(2,1)}, u32[]{:S(2)}) copy-start(bf16[128,128]{1,0:T(8,128)(2,1)} %param.19) | copy-start | bytes 98308
  100.6 41.5 %copy-start.7 = (bf16[128,512]{1,0:T(8,128)(2,1)S(1)}, bf16[128,512]{1,0:T(8,128)(2,1)}, u32[]{:S(2)}) copy-start(bf16[128,512]{1,0:T(8,128)(2,1)} %param.14) | copy-start | bytes 393220
  100.6 41.8 %copy-start.17 = (f32[16]{0:T(128)S(1)}, f32[16]{0:T(128)}, u32[]{:S(2)}) copy-start(f32[16]{0:T(128)} %param.23) | copy-start | bytes 196
  100.7 42.4 %copy-start.18 = (f32[16]{0:T(128)S(1)}, f32[16]{0:T(128)}, u32[]{:S(2)}) copy-start(f32[16]{0:T(128)} %param.22) | copy-start | bytes 196
  100.7 43.1 %copy-start.4 = (bf16[128,1024]{1,0:T(8,128)(2,1)S(1)}, bf16[128,1024]{1,0:T(8,128)(2,1)}, u32[]{:S(2)}) copy-start(bf16[128,1024]{1,0:T(8,128)(2,1)} %param.18) | copy-start | bytes 786436
  100.9 43.7 %copy-start.19 = (f32[16]{0:T(128)S(1)}, f32[16]{0:T(128)}, u32[]{:S(2)}) copy-start(f32[16]{0:T(128)} %param.24) | copy-start | bytes 196
  122.8 40.4 %all-to-all-start.2 = ((bf16[32,128,32]{1,2,0:T(8,128)(2,1)}), bf16[32,128,32]{1,2,0:T(8,128)(2,1)S(1)}, u32[]{:S(2)}, u32[]{:S(2)}) async-start(bf16[32,128,32]{1,2,0:T(8,128)(2,1)} %constant_dynamic-update-slice_fusion), calls=%async_computation.2 | async-start | bytes 524288 | tf_op jit(solution)/shard_map/all_to_all | solution.py:20
  141.1 89.5 %all-gather.8.cloned.1.call-start = ((), (), s32[]{:S(2)}) async-start(), calls=%async_computation.5 | async-start | bytes 3244032 | tf_op jit(solution)/shard_map/all_gather | solution.py:50
  163.2 30.0 %all-to-all-start.3 = ((bf16[128,32,32]{0,2,1:T(8,128)(2,1)}), bf16[128,32,32]{0,2,1:T(8,128)(2,1)}, u32[]{:S(2)}, u32[]{:S(2)}) async-start(bf16[128,32,32]{0,2,1:T(8,128)(2,1)} %bitcast.84), calls=%async_computation.3 | async-start | bytes 524288 | tf_op jit(solution)/shard_map/all_to_all | solution.py:189
  175.6 1.0 copy-start.5
  178.4 0.7 copy-start.6
  179.8 1.0 copy-start.5
  183.9 1.0 copy-start.5
  188.0 1.0 copy-start.5
  193.2 30.0 %all-to-all-start = ((bf16[128,32,16]{0,2,1:T(8,128)(2,1)}), bf16[128,32,16]{0,2,1:T(8,128)(2,1)S(1)}, u32[]{:S(2)}, u32[]{:S(2)}) async-start(bf16[128,32,16]{0,2,1:T(8,128)(2,1)} %bitcast.11), calls=%async_computation | async-start | bytes 262144 | tf_op jit(solution)/shard_map/all_to_all | solution.py:190
  207.4 40.3 %copy-start.1 = (bf16[32,128,32]{1,0,2:T(8,128)(2,1)}, bf16[32,128,32]{1,0,2:T(8,128)(2,1)S(1)}, u32[]{:S(2)}) copy-start(bf16[32,128,32]{1,0,2:T(8,128)(2,1)S(1)} %reshape.317) | copy-start | bytes 786436
  225.0 44.0 %all-to-all-start.1 = ((bf16[32,128,16]{1,2,0:T(8,128)(2,1)}), bf16[32,128,16]{1,2,0:T(8,128)(2,1)}, u32[]{:S(2)}, u32[]{:S(2)}) async-start(bf16[32,128,16]{1,2,0:T(8,128)(2,1)} %copy.214), calls=%async_computation.1 | async-start | bytes 262144 | tf_op jit(solution)/shard_map/all_to_all | solution.py:218
  230.6 1.2 slice-start
  234.8 12.2 %copy-start.9 = (f32[4096,1]{0,1:T(1,128)}, f32[4096,1]{0,1:T(1,128)S(1)}, u32[]{:S(2)}) copy-start(f32[4096,1]{0,1:T(1,128)S(1)} %get-tuple-element.305) | copy-start | bytes 49156
  251.9 3.1 copy-start.8
  255.0 7.1 %copy-start.2 = (bf16[32,128,32]{1,0,2:T(8,128)(2,1)S(1)}, bf16[32,128,32]{1,0,2:T(8,128)(2,1)}, u32[]{:S(2)}) copy-start(bf16[32,128,32]{1,0,2:T(8,128)(2,1)} %copy-done.1) | copy-start | bytes 786436
  255.0 7.1 %copy-start.10 = (f32[4096,1]{0,1:T(1,128)S(1)}, f32[4096,1]{0,1:T(1,128)}, u32[]{:S(2)}) copy-start(f32[4096,1]{0,1:T(1,128)} %copy-done.9) | copy-start | bytes 49156
  255.0 7.1 %copy-start.13 = (pred[128,128]{1,0:T(8,128)(4,1)S(1)}, pred[128,128]{1,0:T(8,128)(4,1)}, u32[]{:S(2)}) copy-start(pred[128,128]{1,0:T(8,128)(4,1)} %iota_compare_fusion) | copy-start | bytes 49156
  262.1 3.6 %copy-start.3 = (bf16[64,64,128]{2,1,0:T(8,128)(2,1)S(1)}, bf16[64,64,128]{2,1,0:T(8,128)(2,1)}, u32[]{:S(2)}) copy-start(bf16[64,64,128]{2,1,0:T(8,128)(2,1)} %pad_maximum_fusion) | copy-start | bytes 3145732
  262.1 3.6 %copy-start.14 = (f32[32,128]{1,0:T(8,128)S(1)}, f32[32,128]{1,0:T(8,128)}, u32[]{:S(2)}) copy-start(f32[32,128]{1,0:T(8,128)} %get-tuple-element.358) | copy-start | bytes 49156
  265.7 38.4 %copy-start.15 = (f32[1024]{0:T(1024)S(1)}, f32[1024]{0:T(1024)}, u32[]{:S(2)}) copy-start(f32[1024]{0:T(1024)} %param.25) | copy-start | bytes 12292
  269.0 34.8 %all-to-all-start.4 = ((bf16[32,128,32]{1,2,0:T(8,128)(2,1)}), bf16[32,128,32]{1,2,0:T(8,128)(2,1)S(1)}, u32[]{:S(2)}, u32[]{:S(2)}) async-start(bf16[32,128,32]{1,2,0:T(8,128)(2,1)} %fusion.48), calls=%async_computation.4 | async-start | bytes 524288 | tf_op jit(solution)/shard_map/all_to_all | solution.py:217
  (3 other events, 2.1 us)
Sparse Core Ops, SparseCore 0:
  74.8 23.9 all-gather.9
  100.9 30.5 all-gather.11
  144.1 84.2 all-gather.7
